TPU v7x, 512 devices: a whole 4x8x8 slice. The times are simulated.
512 devices in a mesh: seq: 256 (over z, x, y_lo, core), head: 2 (over y_hi).
Axes of the slice: x: 4, y: 8 (y_hi: 2, y_lo: 4; y = y_hi * 4 + y_lo), z: 8, core: 2. Of those that a mesh axis runs over, the one named last changes fastest.
Arguments:
- queries: bfloat16 [32768, 2048], P('seq', 'head'), may hold values from -5 to 5
- keys: bfloat16 [32768, 2048], P('seq', 'head'), may hold values from -5 to 5
- values: bfloat16 [32768, 2048], P('seq', 'head'), may hold values from -6 to 6
- grad_out: bfloat16 [32768, 2048], P('seq', 'head'), may hold values from -6 to 6
- doc_ids: int32 [32768], P(('seq', 'head')), may hold values from 0 to 511, never falling along the last dimension, each value on 1 to 512 neighbouring positions
- loss_mask: int32 [32768], P(('seq', 'head')), may hold values 0 or 1
Outputs:
- attended: bfloat16 [32768, 2048], P('seq', 'head')
- query_grad: bfloat16 [32768, 2048], P('seq', 'head')
- key_grad: bfloat16 [32768, 2048], P('seq', 'head')
- value_grad: bfloat16 [32768, 2048], P('seq', 'head')
Inputs may be any that keep to these rules, and one draw needn't show every extreme that they name: `doc_ids`: documents are runs of consecutive tokens numbered 0, 1, 2, ... in order; each has 1 to 512 tokens.
All inputs are finite; a program needn't handle non-finite values. No bound on the sum of `loss_mask` on one device may be relied on, other than what follows from the above.
Results may differ from a plain program's by a relative error of at most 0.033.
Values may be sent and summed in bfloat16 or wider, within the bound.
A program may use at most 64 MiB of HBM per device.

v0:
```python
from functools import reduce
import math
import jax
import jax.numpy as jnp
from jax import lax
from jax.sharding import Mesh
from jax.sharding import PartitionSpec as P

HEAD_DIM = 128
REACH = 4
WINDOW = 512
SEQ = ("seq_0", "seq_1", "seq_2", "seq_3")
SEQ_HEAD = ("seq_0", "seq_1", "seq_2", "seq_3", "head")
masked_value = -1e30
big_index = 2**30


def turned_gather(arrays, axis, dims):
    turned = [jnp.moveaxis(a, dim, 0) for a, dim in zip(arrays, dims)]
    widths = [t[0].size for t in turned]
    both = jnp.concatenate([t.reshape(-1, w) for t, w in zip(turned, widths)], axis=1)
    out = lax.all_gather(both, axis, axis=0, tiled=True)
    pieces = jnp.split(out, [sum(widths[:k]) for k in range(1, len(widths))], axis=1)
    return tuple(
        (
            jnp.moveaxis(b.reshape(-1, *t.shape[1:]), 0, dim)
            for b, t, dim in zip(pieces, turned, dims)
        )
    )


def by_axis(value, axes):
    for axis in axes:
        value = lax.psum(value, axis)
    return value


def one_axis_at_a_time(value, axes):
    for axis in axes:
        value = lax.pmin(value, axis)
    return value


def shifted(block, axis, distance):
    devices = range(lax.axis_size(axis))
    route = [(i - distance, i) for i in devices if i - distance in devices]
    return lax.ppermute(block, axis, route)


def for_sending(value):

    def short(part):
        return part.astype(jnp.bfloat16) if part.dtype == jnp.float32 else part

    return jax.tree.map(short, value)


def allowed_for(q_pos, q_start, k_pos):
    later = k_pos[None, :] <= q_pos[:, None]
    inside = k_pos[None, :] > q_pos[:, None] - WINDOW
    same_doc = k_pos[None, :] >= q_start[:, None]
    return later & inside & same_doc


def by_head(rows):
    return rows.reshape(rows.shape[0], -1, HEAD_DIM)


def tile_scores(q_rows, k_rows, allowed):
    score = jnp.einsum(
        "qhd,khd->hqk", by_head(q_rows), by_head(k_rows), preferred_element_type=jnp.float32
    )
    return jnp.where(allowed[None], score * (1.0 / math.sqrt(HEAD_DIM)), masked_value)


def tile_mix(prob, v_rows):
    return jnp.einsum(
        "hqk,khd->qhd",
        prob.astype(jnp.bfloat16),
        by_head(v_rows),
        preferred_element_type=jnp.float32,
    )


def grad_of_scores(g_rows, v_rows, prob, row_delta):
    prob_grad = jnp.einsum(
        "qhd,khd->hqk", by_head(g_rows), by_head(v_rows), preferred_element_type=jnp.float32
    )
    return (prob * (prob_grad - row_delta[..., None]) * (1.0 / math.sqrt(HEAD_DIM))).astype(
        jnp.bfloat16
    )


def key_terms_of(q_rows, g_rows, k_rows, prob, score_grad):
    key_part = jnp.einsum(
        "hqk,qhd->khd", score_grad, by_head(q_rows), preferred_element_type=jnp.float32
    )
    value_part = jnp.einsum(
        "hqk,qhd->khd",
        prob.astype(jnp.bfloat16),
        by_head(g_rows),
        preferred_element_type=jnp.float32,
    )
    return (key_part.reshape(k_rows.shape), value_part.reshape(k_rows.shape))


def tile_back(q_rows, g_rows, k_rows, v_rows, prob, row_delta):
    score_grad = grad_of_scores(g_rows, v_rows, prob, row_delta)
    result = jnp.einsum(
        "hqk,khd->qhd", score_grad, by_head(k_rows), preferred_element_type=jnp.float32
    )
    key_part, value_part = key_terms_of(q_rows, g_rows, k_rows, prob, score_grad)
    return (result.reshape(q_rows.shape), key_part, value_part)


def body(queries, keys, values, grad_out, doc_ids, loss_mask):
    block_rows, width = queries.shape
    seq_index = lax.axis_index(SEQ)
    doc_rows, mask_rows = turned_gather((doc_ids, loss_mask), "head", (0, 0))
    positions = seq_index * block_rows + jnp.arange(block_rows, dtype=jnp.int32)
    catalog = jnp.arange(2 * lax.axis_size(SEQ), dtype=jnp.int32)
    member = doc_rows[:, None] == catalog[None, :]
    local_counts = jnp.sum(jnp.where(member, mask_rows[:, None].astype(jnp.float32), 0.0), axis=0)
    local_first = jnp.min(jnp.where(member, positions[:, None], big_index), axis=0)
    counts = by_axis(local_counts, SEQ)
    firsts = one_axis_at_a_time(local_first, SEQ)
    doc_start = jnp.sum(jnp.where(member, firsts[None, :], 0), axis=1)
    doc_count = jnp.sum(jnp.where(member, counts[None, :], 0.0), axis=1)
    weight = (
        mask_rows.astype(jnp.float32) * block_rows / jnp.maximum(doc_count, float(block_rows // 8))
    )
    remote = []
    carried = (keys, values)
    for distance in range(1, REACH + 1):
        carried = shifted((carried[0], carried[1]), SEQ, 1)
        remote.append(carried)
    key_blocks = [(keys, values)] + remote
    masks = [
        allowed_for(positions, doc_start, positions - distance * block_rows)
        for distance in range(REACH + 1)
    ]
    score_list = [
        tile_scores(queries, key_blocks[distance][0], masks[distance])
        for distance in range(REACH + 1)
    ]
    row_max = reduce(jnp.maximum, [jnp.max(score, axis=2) for score in score_list])
    row_sum = sum((jnp.sum(jnp.exp(score - row_max[..., None]), axis=2) for score in score_list))
    log_total = row_max + jnp.log(row_sum)
    prob_list = [jnp.exp(score - log_total[..., None]) for score in score_list]
    mixed_out = sum(
        (tile_mix(prob_list[distance], key_blocks[distance][1]) for distance in range(REACH + 1))
    )
    attended = mixed_out.astype(jnp.bfloat16).reshape(block_rows, width)
    grad_rows = (weight[:, None] * grad_out.astype(jnp.float32)).astype(jnp.bfloat16)
    row_delta = jnp.sum(
        by_head(grad_rows).astype(jnp.float32) * by_head(attended).astype(jnp.float32), axis=2
    ).T
    terms = [
        tile_back(
            queries,
            grad_rows,
            key_blocks[distance][0],
            key_blocks[distance][1],
            prob_list[distance],
            row_delta,
        )
        for distance in range(REACH + 1)
    ]
    query_total = sum((term[0] for term in terms))
    carried = (terms[REACH][1], terms[REACH][2])
    for distance in range(REACH - 1, -1, -1):
        carried = shifted((for_sending(carried[0]), for_sending(carried[1])), SEQ, -1)
        carried = (carried[0] + terms[distance][1], carried[1] + terms[distance][2])
    return (
        attended,
        query_total.astype(jnp.bfloat16),
        carried[0].astype(jnp.bfloat16),
        carried[1].astype(jnp.bfloat16),
    )


def solution(mesh):
    torus = Mesh(
        mesh.devices.reshape(8, 4, 4, 2, mesh.shape["head"]),
        ("seq_0", "seq_1", "seq_2", "seq_3", "head"),
    )
    in_specs = (
        P(SEQ, "head"),
        P(SEQ, "head"),
        P(SEQ, "head"),
        P(SEQ, "head"),
        P(SEQ_HEAD),
        P(SEQ_HEAD),
    )
    out_specs = (P(SEQ, "head"), P(SEQ, "head"), P(SEQ, "head"), P(SEQ, "head"))
    return jax.shard_map(body, mesh=torus, in_specs=in_specs, out_specs=out_specs, check_vma=False)
```

profile of v0, /device:TPU:255, one launch (start us, length us, event | category | flops | bytes accessed | tf_op | source)
XLA Modules:
  0.0 208.5 jit_solution(2514917617455026863)
XLA Ops:
  1.8 8.0 %collective-permute-start = (bf16[128,1024]{0,1:T(8,128)(2,1)S(1)}, bf16[128,1024]{0,1:T(8,128)(2,1)S(1)}, u32[]{:S(2)}, u32[]{:S(2)}) collective-permute-start(bf16[128,1024]{0,1:T(8,128)(2,1)S(1)} %copy.331), channel_id=1, source_target_pairs={{0,2},{2,4},{4,6},{6,8},{8,10},{10,12},{12,14},{14,16},{16,18},{18... | collective-permute-start | bytes 786440 | tf_op jit(solution)/shard_map/ppermute | solution.py:47
  9.9 1.9 collective-permute-start.4
  12.6 7.0 %all-gather = s32[2,64,2]{1,2,0:T(2,128)S(1)} all-gather(s32[1,64,2]{1,2,0:T(2,128)S(1)} %add_bitcast_fusion), channel_id=1, replica_groups=mesh['seq_0'=8,'seq_1'=4,'seq_2'=4,'seq_3'=2,'head'=2] {'head'}, dimensions={0}, use_global_device_ids=true | all-gather | bytes 1536 | tf_op jit(solution)/shard_map/all_gather | solution.py:22
  19.8 9.4 %pmin.28 = s32[512]{0:T(512)S(1)} all-reduce(s32[512]{0:T(512)S(1)} %select_reduce_fusion.3), channel_id=1, replica_groups=mesh['seq_0'=8,'seq_1'=4,'seq_2'=4,'seq_3'=2,'head'=2] {'seq_0'}, use_global_device_ids=true, to_apply=%region_1.2 | all-reduce | flops 512 | bytes 4096 | tf_op jit(solution)/shard_map/pmin | solution.py:40
  29.1 5.7 %pmin.29 = s32[512]{0:T(512)S(1)} all-reduce(s32[512]{0:T(512)S(1)} %pmin.28), channel_id=1, replica_groups=mesh['seq_0'=8,'seq_1'=4,'seq_2'=4,'seq_3'=2,'head'=2] {'seq_1'}, use_global_device_ids=true, to_apply=%region_2.3 | all-reduce | flops 512 | bytes 4096 | tf_op jit(solution)/shard_map/pmin | solution.py:40
  34.8 4.0 %pmin.30 = s32[512]{0:T(512)S(1)} all-reduce(s32[512]{0:T(512)S(1)} %pmin.29), channel_id=1, replica_groups=mesh['seq_0'=8,'seq_1'=4,'seq_2'=4,'seq_3'=2,'head'=2] {'seq_2'}, use_global_device_ids=true, to_apply=%region_3.4 | all-reduce | flops 512 | bytes 4096 | tf_op jit(solution)/shard_map/pmin | solution.py:40
  38.8 9.3 %pmin.31 = s32[512]{0:T(512)S(1)} all-reduce(s32[512]{0:T(512)S(1)} %pmin.30), channel_id=1, replica_groups=mesh['seq_0'=8,'seq_1'=4,'seq_2'=4,'seq_3'=2,'head'=2] {'seq_3'}, use_global_device_ids=true, to_apply=%region_4.5 | all-reduce | flops 512 | bytes 4096 | tf_op jit(solution)/shard_map/pmin | solution.py:40
  48.8 10.6 %psum.28 = f32[512]{0:T(512)S(1)} all-reduce(f32[512]{0:T(512)S(1)} %select_reduce_fusion.1), channel_id=1, replica_groups=mesh['seq_0'=8,'seq_1'=4,'seq_2'=4,'seq_3'=2,'head'=2] {'seq_0'}, use_global_device_ids=true, to_apply=%region_17.18 | all-reduce | flops 512 | bytes 4096 | tf_op jit(solution)/shard_map/psum | solution.py:34
  59.4 6.3 %psum.29 = f32[512]{0:T(512)S(1)} all-reduce(f32[512]{0:T(512)S(1)} %psum.28), channel_id=1, replica_groups=mesh['seq_0'=8,'seq_1'=4,'seq_2'=4,'seq_3'=2,'head'=2] {'seq_1'}, use_global_device_ids=true, to_apply=%region_18.19 | all-reduce | flops 512 | bytes 4096 | tf_op jit(solution)/shard_map/psum | solution.py:34
  65.6 7.3 %psum.30 = f32[512]{0:T(512)S(1)} all-reduce(f32[512]{0:T(512)S(1)} %psum.29), channel_id=1, replica_groups=mesh['seq_0'=8,'seq_1'=4,'seq_2'=4,'seq_3'=2,'head'=2] {'seq_2'}, use_global_device_ids=true, to_apply=%region_19.20 | all-reduce | flops 512 | bytes 4096 | tf_op jit(solution)/shard_map/psum | solution.py:34
  72.9 10.1 %psum.31 = f32[512]{0:T(512)S(1)} all-reduce(f32[512]{0:T(512)S(1)} %psum.30), channel_id=1, replica_groups=mesh['seq_0'=8,'seq_1'=4,'seq_2'=4,'seq_3'=2,'head'=2] {'seq_3'}, use_global_device_ids=true, to_apply=%region_20.21 | all-reduce | flops 512 | bytes 4096 | tf_op jit(solution)/shard_map/psum | solution.py:34
  83.4 10.3 %collective-permute-start.1 = (bf16[128,1024]{0,1:T(8,128)(2,1)S(1)}, bf16[128,1024]{0,1:T(8,128)(2,1)S(1)}, u32[]{:S(2)}, u32[]{:S(2)}) collective-permute-start(bf16[128,1024]{0,1:T(8,128)(2,1)S(1)} %collective-permute-done), channel_id=1, source_target_pairs={{0,2},{2,4},{4,6},{6,8},{8,10},{10,12},{12,14},{14,16},{16,18},{18... | collective-permute-start | bytes 786440 | tf_op jit(solution)/shard_map/ppermute | solution.py:47
  93.8 2.1 collective-permute-start.5
  96.9 10.4 %collective-permute-start.2 = (bf16[128,1024]{0,1:T(8,128)(2,1)S(1)}, bf16[128,1024]{0,1:T(8,128)(2,1)}, u32[]{:S(2)}, u32[]{:S(2)}) collective-permute-start(bf16[128,1024]{0,1:T(8,128)(2,1)S(1)} %collective-permute-done.1), channel_id=1, source_target_pairs={{0,2},{2,4},{4,6},{6,8},{8,10},{10,12},{12,14},{14,16},{16,18},{18... | collective-permute-start | bytes 786440 | tf_op jit(solution)/shard_map/ppermute | solution.py:47
  107.6 2.5 %collective-permute-start.6 = (bf16[128,1024]{1,0:T(8,128)(2,1)S(1)}, bf16[128,1024]{1,0:T(8,128)(2,1)}, u32[]{:S(2)}, u32[]{:S(2)}) collective-permute-start(bf16[128,1024]{1,0:T(8,128)(2,1)S(1)} %collective-permute-done.5), channel_id=1, source_target_pairs={{0,2},{2,4},{4,6},{6,8},{8,10},{10,12},{12,14},{14,16},{16,18},{18... | collective-permute-start | bytes 786440 | tf_op jit(solution)/shard_map/ppermute | solution.py:47
  110.6 10.5 %collective-permute-start.3 = (bf16[128,1024]{0,1:T(8,128)(2,1)}, bf16[128,1024]{0,1:T(8,128)(2,1)S(1)}, u32[]{:S(2)}, u32[]{:S(2)}) collective-permute-start(bf16[128,1024]{0,1:T(8,128)(2,1)} %collective-permute-done.2), channel_id=1, source_target_pairs={{0,2},{2,4},{4,6},{6,8},{8,10},{10,12},{12,14},{14,16},{16,18},{18... | collective-permute-start | bytes 786440 | tf_op jit(solution)/shard_map/ppermute | solution.py:47
  122.3 1.8 copy.239
  124.1 1.9 collective-permute-start.7
  135.2 2.1 %multiply_reduce_fusion = (f32[128,8]{0,1:T(8,128)S(1)}, bf16[8,128,128]{1,2,0:T(8,128)(2,1)}) fusion(bf16[128,1024]{0,1:T(8,128)(2,1)S(1)} %copy.243, f32[8,128,128]{1,2,0:T(8,128)} %convolution_add_fusion.5, bf16[128,8,128]{0,2,1:T(8,128)(2,1)} %bitcast.152, f32[8,128,128]{1,2,0:T(8,128)S(1)} %get-tuple-element.33, f32[8,128]{1,0:T(8,128)S(1)} %log_add_fusion), kind=kOutput, calls=%fused_computation.50 | convolution fusion | flops 34601984 | bytes 1843200 | tf_op jit(solution)/shard_map/hqk,khd->qhd/dot_general | solution.py:77
  149.4 2.4 %collective-permute-start.8 = (bf16[128,1024]{1,0:T(8,128)(2,1)S(1)}, bf16[128,1024]{1,0:T(8,128)(2,1)S(1)}, u32[]{:S(2)}, u32[]{:S(2)}) collective-permute-start(bf16[128,1024]{1,0:T(8,128)(2,1)S(1)} %copy.267), channel_id=1, source_target_pairs={{2,0},{4,2},{6,4},{8,6},{10,8},{12,10},{14,12},{16,14},{18,16},{20... | collective-permute-start | bytes 786440 | tf_op jit(solution)/shard_map/ppermute | solution.py:47
  152.3 1.9 collective-permute-start.12
  155.8 7.3 %collective-permute-done.8 = bf16[128,1024]{1,0:T(8,128)(2,1)S(1)} collective-permute-done((bf16[128,1024]{1,0:T(8,128)(2,1)S(1)}, bf16[128,1024]{1,0:T(8,128)(2,1)S(1)}, u32[]{:S(2)}, u32[]{:S(2)}) %collective-permute-start.8) | collective-permute-done | bytes 262176 | tf_op jit(solution)/shard_map/ppermute | solution.py:47
  163.2 2.1 collective-permute-start.9
  166.1 1.9 collective-permute-start.13
  169.6 7.5 %collective-permute-done.9 = bf16[128,1024]{1,0:T(8,128)(2,1)S(1)} collective-permute-done((bf16[128,1024]{1,0:T(8,128)(2,1)S(1)}, bf16[128,1024]{1,0:T(8,128)(2,1)S(1)}, u32[]{:S(2)}, u32[]{:S(2)}) %collective-permute-start.9) | collective-permute-done | bytes 262176 | tf_op jit(solution)/shard_map/ppermute | solution.py:47
  177.1 2.1 collective-permute-start.10
  179.9 1.9 collective-permute-start.14
  183.4 7.6 %collective-permute-done.10 = bf16[128,1024]{1,0:T(8,128)(2,1)S(1)} collective-permute-done((bf16[128,1024]{1,0:T(8,128)(2,1)S(1)}, bf16[128,1024]{1,0:T(8,128)(2,1)S(1)}, u32[]{:S(2)}, u32[]{:S(2)}) %collective-permute-start.10) | collective-permute-done | bytes 262176 | tf_op jit(solution)/shard_map/ppermute | solution.py:47
  191.0 2.1 collective-permute-start.11
  193.9 2.1 collective-permute-start.15
  199.2 5.7 %collective-permute-done.11 = bf16[128,1024]{1,0:T(8,128)(2,1)S(1)} collective-permute-done((bf16[128,1024]{1,0:T(8,128)(2,1)S(1)}, bf16[128,1024]{1,0:T(8,128)(2,1)S(1)}, u32[]{:S(2)}, u32[]{:S(2)}) %collective-permute-start.11) | collective-permute-done | bytes 262176 | tf_op jit(solution)/shard_map/ppermute | solution.py:47
  205.6 2.0 collective-permute-done.15
  (149 shorter events, 39.4 us)
Async XLA Ops:
  0.6 9.3 %copy-start.19 = (bf16[128,1024]{1,0:T(8,128)(2,1)S(1)}, bf16[128,1024]{1,0:T(8,128)(2,1)}, u32[]{:S(2)}) copy-start(bf16[128,1024]{1,0:T(8,128)(2,1)} %param.8) | copy-start | bytes 786436
  0.6 48.0 %copy-start.30 = (bf16[128,1024]{1,0:T(8,128)(2,1)S(1)}, bf16[128,1024]{1,0:T(8,128)(2,1)}, u32[]{:S(2)}) copy-start(bf16[128,1024]{1,0:T(8,128)(2,1)} %param.6) | copy-start | bytes 786436
  1.8 81.2 %copy-start.13 = (bf16[128,1024]{0,1:T(8,128)(2,1)}, bf16[128,1024]{0,1:T(8,128)(2,1)S(1)}, u32[]{:S(2)}) copy-start(bf16[128,1024]{0,1:T(8,128)(2,1)S(1)} %copy.331) | copy-start | bytes 786436
  1.8 81.5 %collective-permute-start = (bf16[128,1024]{0,1:T(8,128)(2,1)S(1)}, bf16[128,1024]{0,1:T(8,128)(2,1)S(1)}, u32[]{:S(2)}, u32[]{:S(2)}) collective-permute-start(bf16[128,1024]{0,1:T(8,128)(2,1)S(1)} %copy.331), channel_id=1, source_target_pairs={{0,2},{2,4},{4,6},{6,8},{8,10},{10,12},{12,14},{14,16},{16,18},{18... | collective-permute-start | bytes 786440 | tf_op jit(solution)/shard_map/ppermute | solution.py:47
  9.9 83.9 %collective-permute-start.4 = (bf16[128,1024]{1,0:T(8,128)(2,1)S(1)}, bf16[128,1024]{1,0:T(8,128)(2,1)S(1)}, u32[]{:S(2)}, u32[]{:S(2)}) collective-permute-start(bf16[128,1024]{1,0:T(8,128)(2,1)S(1)} %copy-done.19), channel_id=1, source_target_pairs={{0,2},{2,4},{4,6},{6,8},{8,10},{10,12},{12,14},{14,16},{16,18},{18... | collective-permute-start | bytes 786440 | tf_op jit(solution)/shard_map/ppermute | solution.py:47
  83.0 24.3 %copy-start.29 = (bf16[128,1024]{1,0:T(8,128)(2,1)S(1)}, bf16[128,1024]{1,0:T(8,128)(2,1)}, u32[]{:S(2)}) copy-start(bf16[128,1024]{1,0:T(8,128)(2,1)} %param.9) | copy-start | bytes 786436
  83.3 26.8 %copy-start.25 = (bf16[128,1024]{0,1:T(8,128)(2,1)}, bf16[128,1024]{0,1:T(8,128)(2,1)S(1)}, u32[]{:S(2)}) copy-start(bf16[128,1024]{0,1:T(8,128)(2,1)S(1)} %collective-permute-done) | copy-start | bytes 786436
  83.4 13.6 %collective-permute-start.1 = (bf16[128,1024]{0,1:T(8,128)(2,1)S(1)}, bf16[128,1024]{0,1:T(8,128)(2,1)S(1)}, u32[]{:S(2)}, u32[]{:S(2)}) collective-permute-start(bf16[128,1024]{0,1:T(8,128)(2,1)S(1)} %collective-permute-done), channel_id=1, source_target_pairs={{0,2},{2,4},{4,6},{6,8},{8,10},{10,12},{12,14},{14,16},{16,18},{18... | collective-permute-start | bytes 786440 | tf_op jit(solution)/shard_map/ppermute | solution.py:47
  93.8 13.8 %collective-permute-start.5 = (bf16[128,1024]{1,0:T(8,128)(2,1)S(1)}, bf16[128,1024]{1,0:T(8,128)(2,1)S(1)}, u32[]{:S(2)}, u32[]{:S(2)}) collective-permute-start(bf16[128,1024]{1,0:T(8,128)(2,1)S(1)} %collective-permute-done.4), channel_id=1, source_target_pairs={{0,2},{2,4},{4,6},{6,8},{8,10},{10,12},{12,14},{14,16},{16,18},{18... | collective-permute-start | bytes 786440 | tf_op jit(solution)/shard_map/ppermute | solution.py:47
  96.9 24.2 %copy-start.27 = (bf16[128,1024]{0,1:T(8,128)(2,1)}, bf16[128,1024]{0,1:T(8,128)(2,1)S(1)}, u32[]{:S(2)}) copy-start(bf16[128,1024]{0,1:T(8,128)(2,1)S(1)} %collective-permute-done.1) | copy-start | bytes 786436
  96.9 13.7 %collective-permute-start.2 = (bf16[128,1024]{0,1:T(8,128)(2,1)S(1)}, bf16[128,1024]{0,1:T(8,128)(2,1)}, u32[]{:S(2)}, u32[]{:S(2)}) collective-permute-start(bf16[128,1024]{0,1:T(8,128)(2,1)S(1)} %collective-permute-done.1), channel_id=1, source_target_pairs={{0,2},{2,4},{4,6},{6,8},{8,10},{10,12},{12,14},{14,16},{16,18},{18... | collective-permute-start | bytes 786440 | tf_op jit(solution)/shard_map/ppermute | solution.py:47
  107.6 14.6 %collective-permute-start.6 = (bf16[128,1024]{1,0:T(8,128)(2,1)S(1)}, bf16[128,1024]{1,0:T(8,128)(2,1)}, u32[]{:S(2)}, u32[]{:S(2)}) collective-permute-start(bf16[128,1024]{1,0:T(8,128)(2,1)S(1)} %collective-permute-done.5), channel_id=1, source_target_pairs={{0,2},{2,4},{4,6},{6,8},{8,10},{10,12},{12,14},{14,16},{16,18},{18... | collective-permute-start | bytes 786440 | tf_op jit(solution)/shard_map/ppermute | solution.py:47
  110.6 16.6 %collective-permute-start.3 = (bf16[128,1024]{0,1:T(8,128)(2,1)}, bf16[128,1024]{0,1:T(8,128)(2,1)S(1)}, u32[]{:S(2)}, u32[]{:S(2)}) collective-permute-start(bf16[128,1024]{0,1:T(8,128)(2,1)} %collective-permute-done.2), channel_id=1, source_target_pairs={{0,2},{2,4},{4,6},{6,8},{8,10},{10,12},{12,14},{14,16},{16,18},{18... | collective-permute-start | bytes 786440 | tf_op jit(solution)/shard_map/ppermute | solution.py:47
  124.1 9.3 %collective-permute-start.7 = (bf16[128,1024]{1,0:T(8,128)(2,1)}, bf16[128,1024]{1,0:T(8,128)(2,1)}, u32[]{:S(2)}, u32[]{:S(2)}) collective-permute-start(bf16[128,1024]{1,0:T(8,128)(2,1)} %collective-permute-done.6), channel_id=1, source_target_pairs={{0,2},{2,4},{4,6},{6,8},{8,10},{10,12},{12,14},{14,16},{16,18},{18... | collective-permute-start | bytes 786440 | tf_op jit(solution)/shard_map/ppermute | solution.py:47
  135.2 2.1 %copy-start.21 = (bf16[128,1024]{1,0:T(8,128)(2,1)S(1)}, bf16[128,1024]{1,0:T(8,128)(2,1)}, u32[]{:S(2)}) copy-start(bf16[128,1024]{1,0:T(8,128)(2,1)} %param.8) | copy-start | bytes 786436
  137.5 7.9 %copy-start.5 = (bf16[8,128,128]{1,2,0:T(8,128)(2,1)}, bf16[8,128,128]{1,2,0:T(8,128)(2,1)S(1)}, u32[]{:S(2)}) copy-start(bf16[8,128,128]{1,2,0:T(8,128)(2,1)S(1)} %fusion.19) | copy-start | bytes 786436
  138.6 7.4 %copy-start.7 = (bf16[8,128,128]{1,2,0:T(8,128)(2,1)}, bf16[8,128,128]{1,2,0:T(8,128)(2,1)S(1)}, u32[]{:S(2)}) copy-start(bf16[8,128,128]{1,2,0:T(8,128)(2,1)S(1)} %fusion.15) | copy-start | bytes 786436
  139.7 7.2 %copy-start.9 = (bf16[8,128,128]{1,2,0:T(8,128)(2,1)}, bf16[8,128,128]{1,2,0:T(8,128)(2,1)S(1)}, u32[]{:S(2)}) copy-start(bf16[8,128,128]{1,2,0:T(8,128)(2,1)S(1)} %fusion.16) | copy-start | bytes 786436
  140.7 7.1 %copy-start.11 = (bf16[8,128,128]{1,2,0:T(8,128)(2,1)}, bf16[8,128,128]{1,2,0:T(8,128)(2,1)S(1)}, u32[]{:S(2)}) copy-start(bf16[8,128,128]{1,2,0:T(8,128)(2,1)S(1)} %fusion.17) | copy-start | bytes 786436
  149.4 13.7 %collective-permute-start.8 = (bf16[128,1024]{1,0:T(8,128)(2,1)S(1)}, bf16[128,1024]{1,0:T(8,128)(2,1)S(1)}, u32[]{:S(2)}, u32[]{:S(2)}) collective-permute-start(bf16[128,1024]{1,0:T(8,128)(2,1)S(1)} %copy.267), channel_id=1, source_target_pairs={{2,0},{4,2},{6,4},{8,6},{10,8},{12,10},{14,12},{16,14},{18,16},{20... | collective-permute-start | bytes 786440 | tf_op jit(solution)/shard_map/ppermute | solution.py:47
  152.2 2.1 %copy-start.12 = (bf16[8,128,128]{1,2,0:T(8,128)(2,1)S(1)}, bf16[8,128,128]{1,2,0:T(8,128)(2,1)}, u32[]{:S(2)}) copy-start(bf16[8,128,128]{1,2,0:T(8,128)(2,1)} %copy-done.11) | copy-start | bytes 786436
  152.3 13.7 %collective-permute-start.12 = (bf16[128,1024]{1,0:T(8,128)(2,1)S(1)}, bf16[128,1024]{1,0:T(8,128)(2,1)S(1)}, u32[]{:S(2)}, u32[]{:S(2)}) collective-permute-start(bf16[128,1024]{1,0:T(8,128)(2,1)S(1)} %copy.281), channel_id=1, source_target_pairs={{2,0},{4,2},{6,4},{8,6},{10,8},{12,10},{14,12},{16,14},{18,16},{20... | collective-permute-start | bytes 786440 | tf_op jit(solution)/shard_map/ppermute | solution.py:47
  163.2 4.8 %copy-start.10 = (bf16[8,128,128]{1,2,0:T(8,128)(2,1)S(1)}, bf16[8,128,128]{1,2,0:T(8,128)(2,1)}, u32[]{:S(2)}) copy-start(bf16[8,128,128]{1,2,0:T(8,128)(2,1)} %copy-done.9) | copy-start | bytes 786436
  163.2 13.8 %collective-permute-start.9 = (bf16[128,1024]{1,0:T(8,128)(2,1)S(1)}, bf16[128,1024]{1,0:T(8,128)(2,1)S(1)}, u32[]{:S(2)}, u32[]{:S(2)}) collective-permute-start(bf16[128,1024]{1,0:T(8,128)(2,1)S(1)} %add_convert_fusion.7), channel_id=1, source_target_pairs={{2,0},{4,2},{6,4},{8,6},{10,8},{12,10},{14,12},{16,14},{18,16},{20... | collective-permute-start | bytes 786440 | tf_op jit(solution)/shard_map/ppermute | solution.py:47
  166.1 13.8 %collective-permute-start.13 = (bf16[128,1024]{1,0:T(8,128)(2,1)S(1)}, bf16[128,1024]{1,0:T(8,128)(2,1)S(1)}, u32[]{:S(2)}, u32[]{:S(2)}) collective-permute-start(bf16[128,1024]{1,0:T(8,128)(2,1)S(1)} %add_convert_fusion.3), channel_id=1, source_target_pairs={{2,0},{4,2},{6,4},{8,6},{10,8},{12,10},{14,12},{16,14},{18,16},{20... | collective-permute-start | bytes 786440 | tf_op jit(solution)/shard_map/ppermute | solution.py:47
  177.1 4.7 %copy-start.8 = (bf16[8,128,128]{1,2,0:T(8,128)(2,1)S(1)}, bf16[8,128,128]{1,2,0:T(8,128)(2,1)}, u32[]{:S(2)}) copy-start(bf16[8,128,128]{1,2,0:T(8,128)(2,1)} %copy-done.7) | copy-start | bytes 786436
  177.1 13.8 %collective-permute-start.10 = (bf16[128,1024]{1,0:T(8,128)(2,1)S(1)}, bf16[128,1024]{1,0:T(8,128)(2,1)S(1)}, u32[]{:S(2)}, u32[]{:S(2)}) collective-permute-start(bf16[128,1024]{1,0:T(8,128)(2,1)S(1)} %add_convert_fusion.6), channel_id=1, source_target_pairs={{2,0},{4,2},{6,4},{8,6},{10,8},{12,10},{14,12},{16,14},{18,16},{20... | collective-permute-start | bytes 786440 | tf_op jit(solution)/shard_map/ppermute | solution.py:47
  179.9 13.9 %collective-permute-start.14 = (bf16[128,1024]{1,0:T(8,128)(2,1)S(1)}, bf16[128,1024]{1,0:T(8,128)(2,1)S(1)}, u32[]{:S(2)}, u32[]{:S(2)}) collective-permute-start(bf16[128,1024]{1,0:T(8,128)(2,1)S(1)} %add_convert_fusion.2), channel_id=1, source_target_pairs={{2,0},{4,2},{6,4},{8,6},{10,8},{12,10},{14,12},{16,14},{18,16},{20... | collective-permute-start | bytes 786440 | tf_op jit(solution)/shard_map/ppermute | solution.py:47
  191.0 4.9 %copy-start.6 = (bf16[8,128,128]{1,2,0:T(8,128)(2,1)S(1)}, bf16[8,128,128]{1,2,0:T(8,128)(2,1)}, u32[]{:S(2)}) copy-start(bf16[8,128,128]{1,2,0:T(8,128)(2,1)} %copy-done.5) | copy-start | bytes 786436
  191.0 13.8 %collective-permute-start.11 = (bf16[128,1024]{1,0:T(8,128)(2,1)S(1)}, bf16[128,1024]{1,0:T(8,128)(2,1)S(1)}, u32[]{:S(2)}, u32[]{:S(2)}) collective-permute-start(bf16[128,1024]{1,0:T(8,128)(2,1)S(1)} %add_convert_fusion.5), channel_id=1, source_target_pairs={{2,0},{4,2},{6,4},{8,6},{10,8},{12,10},{14,12},{16,14},{18,16},{20... | collective-permute-start | bytes 786440 | tf_op jit(solution)/shard_map/ppermute | solution.py:47
  193.8 2.4 %copy-start.22 = (bf16[8,128,128]{1,2,0:T(8,128)(2,1)S(1)}, bf16[8,128,128]{1,2,0:T(8,128)(2,1)}, u32[]{:S(2)}) copy-start(bf16[8,128,128]{1,2,0:T(8,128)(2,1)} %get-tuple-element.43) | copy-start | bytes 786436
  193.9 13.8 %collective-permute-start.15 = (bf16[128,1024]{1,0:T(8,128)(2,1)S(1)}, bf16[128,1024]{1,0:T(8,128)(2,1)S(1)}, u32[]{:S(2)}, u32[]{:S(2)}) collective-permute-start(bf16[128,1024]{1,0:T(8,128)(2,1)S(1)} %add_convert_fusion.1), channel_id=1, source_target_pairs={{2,0},{4,2},{6,4},{8,6},{10,8},{12,10},{14,12},{16,14},{18,16},{20... | collective-permute-start | bytes 786440 | tf_op jit(solution)/shard_map/ppermute | solution.py:47
  (17 other events, 16.5 us)
where the time goes:
time: 210 us; the launch traced here: 208 us
  blocking collectives  69.6 us (33%)
  starting transfers between devices  64 us (30%)
  waiting for transfers between devices  33.2 us (16%)
  local copies, waits for them, and re-layouts  20 us (10%)
  matrix products  17 us (8%)
  other arithmetic  3.2 us (2%)
    ppermute x16, starting transfers between devices, shifted(): return lax.ppermute(block, axis, route)  64 us
    psum x4, blocking collectives, by_axis(): value = lax.psum(value, axis)  34.3 us
    ppermute x16, waiting for transfers between devices, shifted(): return lax.ppermute(block, axis, route)  33.2 us
    pmin x4, blocking collectives, one_axis_at_a_time(): value = lax.pmin(value, axis)  28.4 us
    unnamed x69, local copies, waits for them, and re-layouts  12 us
    all_gather x1, blocking collectives, turned_gather(): out = lax.all_gather(both, axis, axis=0, tiled=True)  6.99 us
    dot_general x5, matrix products, key_terms_of(): jnp.einsum('hqk,qhd->khd', prob.astype(jnp.bfloat16), by_head(g_rows), pr...  4.77 us
    ppermute x4, local copies, waits for them, and re-layouts, shifted(): return lax.ppermute(block, axis, route)  4.59 us
  transfers between devices with their start and end apart: 16, of which 9 were waited for; matrix products, arithmetic and copies ran while one was open for 8% of the time, Pallas kernels for 0%

commit v1 on v0

--- a/solution.py
+++ b/solution.py
@@ -31,7 +31,7 @@
 
 def by_axis(value, axes):
     for axis in axes:
-        value = lax.psum(value, axis)
+        value = jnp.sum(lax.all_gather(value, axis_name=axis), axis=0)
     return value
 
 

time: 210 us -> 220 us (1.048)
  blocking collectives: 69.6 us -> 80.3 us
  starting transfers between devices: 64 us -> 61.7 us
    all_gather x0 -> x4, blocking collectives: none -> 44.9 us  [by_axis(): value = jnp.sum(lax.all_gather(value, axis_name=axis), axis=0)]
    psum x4 -> x0, blocking collectives: 34.3 us -> none  [by_axis(): value = lax.psum(value, axis)]
    ppermute x16, starting transfers between devices: 64 us -> 61.7 us  [shifted(): return lax.ppermute(block, axis, route)]
where the time goes in v1:
time: 220 us; the launch traced here: 218 us
  blocking collectives  80.3 us (36%)
  starting transfers between devices  61.7 us (28%)
  waiting for transfers between devices  33.3 us (15%)
  local copies, waits for them, and re-layouts  19.3 us (9%)
  matrix products  17 us (8%)
  other arithmetic  5.21 us (2%)
    ppermute x16, starting transfers between devices, shifted(): return lax.ppermute(block, axis, route)  61.7 us
    all_gather x4, blocking collectives, by_axis(): value = jnp.sum(lax.all_gather(value, axis_name=axis), axis=0)  44.9 us
    ppermute x16, waiting for transfers between devices, shifted(): return lax.ppermute(block, axis, route)  33.3 us
    pmin x4, blocking collectives, one_axis_at_a_time(): value = lax.pmin(value, axis)  28.4 us
    unnamed x69, local copies, waits for them, and re-layouts  11.4 us
    all_gather x1, blocking collectives, turned_gather(): out = lax.all_gather(both, axis, axis=0, tiled=True)  7 us
    dot_general x5, matrix products, key_terms_of(): jnp.einsum('hqk,qhd->khd', prob.astype(jnp.bfloat16), by_head(g_rows), pr...  4.77 us
    ppermute x4, local copies, waits for them, and re-layouts, shifted(): return lax.ppermute(block, axis, route)  4.59 us
  transfers between devices with their start and end apart: 16, of which 9 were waited for; matrix products, arithmetic and copies ran while one was open for 8% of the time, Pallas kernels for 0%

profile of v1, /device:TPU:255, one launch (start us, length us, event | category | flops | bytes accessed | tf_op | source)
XLA Modules:
  0.0 218.3 jit_solution(2736696348433483805)
XLA Ops:
  1.8 8.2 %collective-permute-start = (bf16[128,1024]{0,1:T(8,128)(2,1)S(1)}, bf16[128,1024]{0,1:T(8,128)(2,1)S(1)}, u32[]{:S(2)}, u32[]{:S(2)}) collective-permute-start(bf16[128,1024]{0,1:T(8,128)(2,1)S(1)} %copy.331), channel_id=1, source_target_pairs={{0,2},{2,4},{4,6},{6,8},{8,10},{10,12},{12,14},{14,16},{16,18},{18... | collective-permute-start | bytes 786440 | tf_op jit(solution)/shard_map/ppermute | solution.py:47
  10.0 1.9 collective-permute-start.4
  12.1 7.0 %all-gather.4 = s32[2,64,2]{1,2,0:T(2,128)S(1)} all-gather(s32[1,64,2]{1,2,0:T(2,128)S(1)} %add_bitcast_fusion), channel_id=1, replica_groups=mesh['seq_0'=8,'seq_1'=4,'seq_2'=4,'seq_3'=2,'head'=2] {'head'}, dimensions={0}, use_global_device_ids=true | all-gather | bytes 1536 | tf_op jit(solution)/shard_map/all_gather | solution.py:22
  19.4 9.4 %pmin.28 = s32[512]{0:T(512)S(1)} all-reduce(s32[512]{0:T(512)S(1)} %select_reduce_fusion.3), channel_id=1, replica_groups=mesh['seq_0'=8,'seq_1'=4,'seq_2'=4,'seq_3'=2,'head'=2] {'seq_0'}, use_global_device_ids=true, to_apply=%region_1.2 | all-reduce | flops 512 | bytes 4096 | tf_op jit(solution)/shard_map/pmin | solution.py:40
  28.7 5.7 %pmin.29 = s32[512]{0:T(512)S(1)} all-reduce(s32[512]{0:T(512)S(1)} %pmin.28), channel_id=1, replica_groups=mesh['seq_0'=8,'seq_1'=4,'seq_2'=4,'seq_3'=2,'head'=2] {'seq_1'}, use_global_device_ids=true, to_apply=%region_2.3 | all-reduce | flops 512 | bytes 4096 | tf_op jit(solution)/shard_map/pmin | solution.py:40
  34.4 4.0 %pmin.30 = s32[512]{0:T(512)S(1)} all-reduce(s32[512]{0:T(512)S(1)} %pmin.29), channel_id=1, replica_groups=mesh['seq_0'=8,'seq_1'=4,'seq_2'=4,'seq_3'=2,'head'=2] {'seq_2'}, use_global_device_ids=true, to_apply=%region_3.4 | all-reduce | flops 512 | bytes 4096 | tf_op jit(solution)/shard_map/pmin | solution.py:40
  38.4 9.3 %pmin.31 = s32[512]{0:T(512)S(1)} all-reduce(s32[512]{0:T(512)S(1)} %pmin.30), channel_id=1, replica_groups=mesh['seq_0'=8,'seq_1'=4,'seq_2'=4,'seq_3'=2,'head'=2] {'seq_3'}, use_global_device_ids=true, to_apply=%region_4.5 | all-reduce | flops 512 | bytes 4096 | tf_op jit(solution)/shard_map/pmin | solution.py:40
  48.1 15.2 %all-gather.5 = f32[8,1,512]{2,1,0:T(1,128)S(1)} all-gather(f32[1,1,512]{2,1,0:T(1,128)S(1)} %bitcast.184), channel_id=2, replica_groups=mesh['seq_0'=8,'seq_1'=4,'seq_2'=4,'seq_3'=2,'head'=2] {'seq_0'}, dimensions={0}, use_global_device_ids=true | all-gather | bytes 18432 | tf_op jit(solution)/shard_map/all_gather | solution.py:34
  63.4 7.3 %all-gather.6 = f32[4,1,512]{2,1,0:T(1,128)S(1)} all-gather(f32[1,1,512]{2,1,0:T(1,128)S(1)} %bitcast.183), channel_id=3, replica_groups=mesh['seq_0'=8,'seq_1'=4,'seq_2'=4,'seq_3'=2,'head'=2] {'seq_1'}, dimensions={0}, use_global_device_ids=true | all-gather | bytes 10240 | tf_op jit(solution)/shard_map/all_gather | solution.py:34
  70.7 9.3 %all-gather.7 = f32[4,1,512]{2,1,0:T(1,128)S(1)} all-gather(f32[1,1,512]{2,1,0:T(1,128)S(1)} %bitcast.185), channel_id=4, replica_groups=mesh['seq_0'=8,'seq_1'=4,'seq_2'=4,'seq_3'=2,'head'=2] {'seq_2'}, dimensions={0}, use_global_device_ids=true | all-gather | bytes 10240 | tf_op jit(solution)/shard_map/all_gather | solution.py:34
  80.0 13.1 %all-gather.8 = f32[2,1,512]{2,1,0:T(1,128)S(1)} all-gather(f32[1,1,512]{2,1,0:T(1,128)S(1)} %bitcast.186), channel_id=5, replica_groups=mesh['seq_0'=8,'seq_1'=4,'seq_2'=4,'seq_3'=2,'head'=2] {'seq_3'}, dimensions={0}, use_global_device_ids=true | all-gather | bytes 6144 | tf_op jit(solution)/shard_map/all_gather | solution.py:34
  93.6 7.8 %collective-permute-start.1 = (bf16[128,1024]{0,1:T(8,128)(2,1)S(1)}, bf16[128,1024]{0,1:T(8,128)(2,1)S(1)}, u32[]{:S(2)}, u32[]{:S(2)}) collective-permute-start(bf16[128,1024]{0,1:T(8,128)(2,1)S(1)} %collective-permute-done), channel_id=1, source_target_pairs={{0,2},{2,4},{4,6},{6,8},{8,10},{10,12},{12,14},{14,16},{16,18},{18... | collective-permute-start | bytes 786440 | tf_op jit(solution)/shard_map/ppermute | solution.py:47
  101.7 2.1 collective-permute-start.5
  104.8 10.4 %collective-permute-start.2 = (bf16[128,1024]{0,1:T(8,128)(2,1)S(1)}, bf16[128,1024]{0,1:T(8,128)(2,1)}, u32[]{:S(2)}, u32[]{:S(2)}) collective-permute-start(bf16[128,1024]{0,1:T(8,128)(2,1)S(1)} %collective-permute-done.1), channel_id=1, source_target_pairs={{0,2},{2,4},{4,6},{6,8},{8,10},{10,12},{12,14},{14,16},{16,18},{18... | collective-permute-start | bytes 786440 | tf_op jit(solution)/shard_map/ppermute | solution.py:47
  115.5 2.5 %collective-permute-start.6 = (bf16[128,1024]{1,0:T(8,128)(2,1)S(1)}, bf16[128,1024]{1,0:T(8,128)(2,1)}, u32[]{:S(2)}, u32[]{:S(2)}) collective-permute-start(bf16[128,1024]{1,0:T(8,128)(2,1)S(1)} %collective-permute-done.5), channel_id=1, source_target_pairs={{0,2},{2,4},{4,6},{6,8},{8,10},{10,12},{12,14},{14,16},{16,18},{18... | collective-permute-start | bytes 786440 | tf_op jit(solution)/shard_map/ppermute | solution.py:47
  118.5 10.5 %collective-permute-start.3 = (bf16[128,1024]{0,1:T(8,128)(2,1)}, bf16[128,1024]{0,1:T(8,128)(2,1)S(1)}, u32[]{:S(2)}, u32[]{:S(2)}) collective-permute-start(bf16[128,1024]{0,1:T(8,128)(2,1)} %collective-permute-done.2), channel_id=1, source_target_pairs={{0,2},{2,4},{4,6},{6,8},{8,10},{10,12},{12,14},{14,16},{16,18},{18... | collective-permute-start | bytes 786440 | tf_op jit(solution)/shard_map/ppermute | solution.py:47
  130.1 1.8 copy.239
  131.9 1.9 collective-permute-start.7
  143.0 2.1 multiply_reduce_fusion
  157.3 2.4 %collective-permute-start.8 = (bf16[128,1024]{1,0:T(8,128)(2,1)S(1)}, bf16[128,1024]{1,0:T(8,128)(2,1)S(1)}, u32[]{:S(2)}, u32[]{:S(2)}) collective-permute-start(bf16[128,1024]{1,0:T(8,128)(2,1)S(1)} %copy.267), channel_id=1, source_target_pairs={{2,0},{4,2},{6,4},{8,6},{10,8},{12,10},{14,12},{16,14},{18,16},{20... | collective-permute-start | bytes 786440 | tf_op jit(solution)/shard_map/ppermute | solution.py:47
  160.2 1.9 collective-permute-start.12
  163.7 7.3 %collective-permute-done.8 = bf16[128,1024]{1,0:T(8,128)(2,1)S(1)} collective-permute-done((bf16[128,1024]{1,0:T(8,128)(2,1)S(1)}, bf16[128,1024]{1,0:T(8,128)(2,1)S(1)}, u32[]{:S(2)}, u32[]{:S(2)}) %collective-permute-start.8) | collective-permute-done | bytes 262176 | tf_op jit(solution)/shard_map/ppermute | solution.py:47
  171.1 2.1 collective-permute-start.9
  174.0 1.9 collective-permute-start.13
  177.4 7.5 %collective-permute-done.9 = bf16[128,1024]{1,0:T(8,128)(2,1)S(1)} collective-permute-done((bf16[128,1024]{1,0:T(8,128)(2,1)S(1)}, bf16[128,1024]{1,0:T(8,128)(2,1)S(1)}, u32[]{:S(2)}, u32[]{:S(2)}) %collective-permute-start.9) | collective-permute-done | bytes 262176 | tf_op jit(solution)/shard_map/ppermute | solution.py:47
  185.0 2.1 collective-permute-start.10
  188.8 1.9 collective-permute-start.14
  192.3 6.5 %collective-permute-done.10 = bf16[128,1024]{1,0:T(8,128)(2,1)S(1)} collective-permute-done((bf16[128,1024]{1,0:T(8,128)(2,1)S(1)}, bf16[128,1024]{1,0:T(8,128)(2,1)S(1)}, u32[]{:S(2)}, u32[]{:S(2)}) %collective-permute-start.10) | collective-permute-done | bytes 262176 | tf_op jit(solution)/shard_map/ppermute | solution.py:47
  198.9 2.1 collective-permute-start.11
  203.7 2.1 collective-permute-start.15
  209.0 3.7 %collective-permute-done.11 = bf16[128,1024]{1,0:T(8,128)(2,1)S(1)} collective-permute-done((bf16[128,1024]{1,0:T(8,128)(2,1)S(1)}, bf16[128,1024]{1,0:T(8,128)(2,1)S(1)}, u32[]{:S(2)}, u32[]{:S(2)}) %collective-permute-start.11) | collective-permute-done | bytes 262176 | tf_op jit(solution)/shard_map/ppermute | solution.py:47
  213.5 4.0 %collective-permute-done.15 = bf16[128,1024]{1,0:T(8,128)(2,1)S(1)} collective-permute-done((bf16[128,1024]{1,0:T(8,128)(2,1)S(1)}, bf16[128,1024]{1,0:T(8,128)(2,1)S(1)}, u32[]{:S(2)}, u32[]{:S(2)}) %collective-permute-start.15) | collective-permute-done | bytes 262176 | tf_op jit(solution)/shard_map/ppermute | solution.py:47
  (153 shorter events, 41.8 us)
Async XLA Ops:
  0.6 9.4 %copy-start.19 = (bf16[128,1024]{1,0:T(8,128)(2,1)S(1)}, bf16[128,1024]{1,0:T(8,128)(2,1)}, u32[]{:S(2)}) copy-start(bf16[128,1024]{1,0:T(8,128)(2,1)} %param.8) | copy-start | bytes 786436
  0.6 11.4 %copy-start.31 = (s32[64]{0:T(128)S(1)}, s32[64]{0:T(128)}, u32[]{:S(2)}) copy-start(s32[64]{0:T(128)} %param.11) | copy-start | bytes 772
  0.7 11.4 %copy-start.32 = (s32[64]{0:T(128)S(1)}, s32[64]{0:T(128)}, u32[]{:S(2)}) copy-start(s32[64]{0:T(128)} %param.10) | copy-start | bytes 772
  1.8 91.5 %copy-start.13 = (bf16[128,1024]{0,1:T(8,128)(2,1)}, bf16[128,1024]{0,1:T(8,128)(2,1)S(1)}, u32[]{:S(2)}) copy-start(bf16[128,1024]{0,1:T(8,128)(2,1)S(1)} %copy.331) | copy-start | bytes 786436
  1.8 91.3 %copy-start.30 = (bf16[128,1024]{1,0:T(8,128)(2,1)S(1)}, bf16[128,1024]{1,0:T(8,128)(2,1)}, u32[]{:S(2)}) copy-start(bf16[128,1024]{1,0:T(8,128)(2,1)} %param.6) | copy-start | bytes 786436
  1.8 91.8 %collective-permute-start = (bf16[128,1024]{0,1:T(8,128)(2,1)S(1)}, bf16[128,1024]{0,1:T(8,128)(2,1)S(1)}, u32[]{:S(2)}, u32[]{:S(2)}) collective-permute-start(bf16[128,1024]{0,1:T(8,128)(2,1)S(1)} %copy.331), channel_id=1, source_target_pairs={{0,2},{2,4},{4,6},{6,8},{8,10},{10,12},{12,14},{14,16},{16,18},{18... | collective-permute-start | bytes 786440 | tf_op jit(solution)/shard_map/ppermute | solution.py:47
  10.0 91.6 %collective-permute-start.4 = (bf16[128,1024]{1,0:T(8,128)(2,1)S(1)}, bf16[128,1024]{1,0:T(8,128)(2,1)S(1)}, u32[]{:S(2)}, u32[]{:S(2)}) collective-permute-start(bf16[128,1024]{1,0:T(8,128)(2,1)S(1)} %copy-done.19), channel_id=1, source_target_pairs={{0,2},{2,4},{4,6},{6,8},{8,10},{10,12},{12,14},{14,16},{16,18},{18... | collective-permute-start | bytes 786440 | tf_op jit(solution)/shard_map/ppermute | solution.py:47
  93.3 21.9 %copy-start.29 = (bf16[128,1024]{1,0:T(8,128)(2,1)S(1)}, bf16[128,1024]{1,0:T(8,128)(2,1)}, u32[]{:S(2)}) copy-start(bf16[128,1024]{1,0:T(8,128)(2,1)} %param.9) | copy-start | bytes 786436
  93.6 24.4 %copy-start.25 = (bf16[128,1024]{0,1:T(8,128)(2,1)}, bf16[128,1024]{0,1:T(8,128)(2,1)S(1)}, u32[]{:S(2)}) copy-start(bf16[128,1024]{0,1:T(8,128)(2,1)S(1)} %collective-permute-done) | copy-start | bytes 786436
  93.6 11.1 %collective-permute-start.1 = (bf16[128,1024]{0,1:T(8,128)(2,1)S(1)}, bf16[128,1024]{0,1:T(8,128)(2,1)S(1)}, u32[]{:S(2)}, u32[]{:S(2)}) collective-permute-start(bf16[128,1024]{0,1:T(8,128)(2,1)S(1)} %collective-permute-done), channel_id=1, source_target_pairs={{0,2},{2,4},{4,6},{6,8},{8,10},{10,12},{12,14},{14,16},{16,18},{18... | collective-permute-start | bytes 786440 | tf_op jit(solution)/shard_map/ppermute | solution.py:47
  101.7 13.8 %collective-permute-start.5 = (bf16[128,1024]{1,0:T(8,128)(2,1)S(1)}, bf16[128,1024]{1,0:T(8,128)(2,1)S(1)}, u32[]{:S(2)}, u32[]{:S(2)}) collective-permute-start(bf16[128,1024]{1,0:T(8,128)(2,1)S(1)} %collective-permute-done.4), channel_id=1, source_target_pairs={{0,2},{2,4},{4,6},{6,8},{8,10},{10,12},{12,14},{14,16},{16,18},{18... | collective-permute-start | bytes 786440 | tf_op jit(solution)/shard_map/ppermute | solution.py:47
  104.8 24.2 %copy-start.27 = (bf16[128,1024]{0,1:T(8,128)(2,1)}, bf16[128,1024]{0,1:T(8,128)(2,1)S(1)}, u32[]{:S(2)}) copy-start(bf16[128,1024]{0,1:T(8,128)(2,1)S(1)} %collective-permute-done.1) | copy-start | bytes 786436
  104.8 13.7 %collective-permute-start.2 = (bf16[128,1024]{0,1:T(8,128)(2,1)S(1)}, bf16[128,1024]{0,1:T(8,128)(2,1)}, u32[]{:S(2)}, u32[]{:S(2)}) collective-permute-start(bf16[128,1024]{0,1:T(8,128)(2,1)S(1)} %collective-permute-done.1), channel_id=1, source_target_pairs={{0,2},{2,4},{4,6},{6,8},{8,10},{10,12},{12,14},{14,16},{16,18},{18... | collective-permute-start | bytes 786440 | tf_op jit(solution)/shard_map/ppermute | solution.py:47
  115.5 14.6 %collective-permute-start.6 = (bf16[128,1024]{1,0:T(8,128)(2,1)S(1)}, bf16[128,1024]{1,0:T(8,128)(2,1)}, u32[]{:S(2)}, u32[]{:S(2)}) collective-permute-start(bf16[128,1024]{1,0:T(8,128)(2,1)S(1)} %collective-permute-done.5), channel_id=1, source_target_pairs={{0,2},{2,4},{4,6},{6,8},{8,10},{10,12},{12,14},{14,16},{16,18},{18... | collective-permute-start | bytes 786440 | tf_op jit(solution)/shard_map/ppermute | solution.py:47
  118.5 16.6 %collective-permute-start.3 = (bf16[128,1024]{0,1:T(8,128)(2,1)}, bf16[128,1024]{0,1:T(8,128)(2,1)S(1)}, u32[]{:S(2)}, u32[]{:S(2)}) collective-permute-start(bf16[128,1024]{0,1:T(8,128)(2,1)} %collective-permute-done.2), channel_id=1, source_target_pairs={{0,2},{2,4},{4,6},{6,8},{8,10},{10,12},{12,14},{14,16},{16,18},{18... | collective-permute-start | bytes 786440 | tf_op jit(solution)/shard_map/ppermute | solution.py:47
  131.9 9.3 %collective-permute-start.7 = (bf16[128,1024]{1,0:T(8,128)(2,1)}, bf16[128,1024]{1,0:T(8,128)(2,1)}, u32[]{:S(2)}, u32[]{:S(2)}) collective-permute-start(bf16[128,1024]{1,0:T(8,128)(2,1)} %collective-permute-done.6), channel_id=1, source_target_pairs={{0,2},{2,4},{4,6},{6,8},{8,10},{10,12},{12,14},{14,16},{16,18},{18... | collective-permute-start | bytes 786440 | tf_op jit(solution)/shard_map/ppermute | solution.py:47
  145.4 7.9 %copy-start.5 = (bf16[8,128,128]{1,2,0:T(8,128)(2,1)}, bf16[8,128,128]{1,2,0:T(8,128)(2,1)S(1)}, u32[]{:S(2)}) copy-start(bf16[8,128,128]{1,2,0:T(8,128)(2,1)S(1)} %fusion.19) | copy-start | bytes 786436
  146.5 7.4 %copy-start.7 = (bf16[8,128,128]{1,2,0:T(8,128)(2,1)}, bf16[8,128,128]{1,2,0:T(8,128)(2,1)S(1)}, u32[]{:S(2)}) copy-start(bf16[8,128,128]{1,2,0:T(8,128)(2,1)S(1)} %fusion.15) | copy-start | bytes 786436
  147.5 7.2 %copy-start.9 = (bf16[8,128,128]{1,2,0:T(8,128)(2,1)}, bf16[8,128,128]{1,2,0:T(8,128)(2,1)S(1)}, u32[]{:S(2)}) copy-start(bf16[8,128,128]{1,2,0:T(8,128)(2,1)S(1)} %fusion.16) | copy-start | bytes 786436
  148.6 7.1 %copy-start.11 = (bf16[8,128,128]{1,2,0:T(8,128)(2,1)}, bf16[8,128,128]{1,2,0:T(8,128)(2,1)S(1)}, u32[]{:S(2)}) copy-start(bf16[8,128,128]{1,2,0:T(8,128)(2,1)S(1)} %fusion.17) | copy-start | bytes 786436
  157.3 13.7 %collective-permute-start.8 = (bf16[128,1024]{1,0:T(8,128)(2,1)S(1)}, bf16[128,1024]{1,0:T(8,128)(2,1)S(1)}, u32[]{:S(2)}, u32[]{:S(2)}) collective-permute-start(bf16[128,1024]{1,0:T(8,128)(2,1)S(1)} %copy.267), channel_id=1, source_target_pairs={{2,0},{4,2},{6,4},{8,6},{10,8},{12,10},{14,12},{16,14},{18,16},{20... | collective-permute-start | bytes 786440 | tf_op jit(solution)/shard_map/ppermute | solution.py:47
  160.2 13.7 %collective-permute-start.12 = (bf16[128,1024]{1,0:T(8,128)(2,1)S(1)}, bf16[128,1024]{1,0:T(8,128)(2,1)S(1)}, u32[]{:S(2)}, u32[]{:S(2)}) collective-permute-start(bf16[128,1024]{1,0:T(8,128)(2,1)S(1)} %copy.281), channel_id=1, source_target_pairs={{2,0},{4,2},{6,4},{8,6},{10,8},{12,10},{14,12},{16,14},{18,16},{20... | collective-permute-start | bytes 786440 | tf_op jit(solution)/shard_map/ppermute | solution.py:47
  171.1 4.8 %copy-start.10 = (bf16[8,128,128]{1,2,0:T(8,128)(2,1)S(1)}, bf16[8,128,128]{1,2,0:T(8,128)(2,1)}, u32[]{:S(2)}) copy-start(bf16[8,128,128]{1,2,0:T(8,128)(2,1)} %copy-done.9) | copy-start | bytes 786436
  171.1 13.8 %collective-permute-start.9 = (bf16[128,1024]{1,0:T(8,128)(2,1)S(1)}, bf16[128,1024]{1,0:T(8,128)(2,1)S(1)}, u32[]{:S(2)}, u32[]{:S(2)}) collective-permute-start(bf16[128,1024]{1,0:T(8,128)(2,1)S(1)} %add_convert_fusion.7), channel_id=1, source_target_pairs={{2,0},{4,2},{6,4},{8,6},{10,8},{12,10},{14,12},{16,14},{18,16},{20... | collective-permute-start | bytes 786440 | tf_op jit(solution)/shard_map/ppermute | solution.py:47
  174.0 13.9 %collective-permute-start.13 = (bf16[128,1024]{1,0:T(8,128)(2,1)S(1)}, bf16[128,1024]{1,0:T(8,128)(2,1)}, u32[]{:S(2)}, u32[]{:S(2)}) collective-permute-start(bf16[128,1024]{1,0:T(8,128)(2,1)S(1)} %add_convert_fusion.3), channel_id=1, source_target_pairs={{2,0},{4,2},{6,4},{8,6},{10,8},{12,10},{14,12},{16,14},{18,16},{20... | collective-permute-start | bytes 786440 | tf_op jit(solution)/shard_map/ppermute | solution.py:47
  185.0 5.8 %copy-start.8 = (bf16[8,128,128]{1,2,0:T(8,128)(2,1)S(1)}, bf16[8,128,128]{1,2,0:T(8,128)(2,1)}, u32[]{:S(2)}) copy-start(bf16[8,128,128]{1,2,0:T(8,128)(2,1)} %copy-done.7) | copy-start | bytes 786436
  185.0 13.8 %collective-permute-start.10 = (bf16[128,1024]{1,0:T(8,128)(2,1)S(1)}, bf16[128,1024]{1,0:T(8,128)(2,1)S(1)}, u32[]{:S(2)}, u32[]{:S(2)}) collective-permute-start(bf16[128,1024]{1,0:T(8,128)(2,1)S(1)} %add_convert_fusion.6), channel_id=1, source_target_pairs={{2,0},{4,2},{6,4},{8,6},{10,8},{12,10},{14,12},{16,14},{18,16},{20... | collective-permute-start | bytes 786440 | tf_op jit(solution)/shard_map/ppermute | solution.py:47
  188.8 13.8 %collective-permute-start.14 = (bf16[128,1024]{1,0:T(8,128)(2,1)S(1)}, bf16[128,1024]{1,0:T(8,128)(2,1)}, u32[]{:S(2)}, u32[]{:S(2)}) collective-permute-start(bf16[128,1024]{1,0:T(8,128)(2,1)S(1)} %add_convert_fusion.2), channel_id=1, source_target_pairs={{2,0},{4,2},{6,4},{8,6},{10,8},{12,10},{14,12},{16,14},{18,16},{20... | collective-permute-start | bytes 786440 | tf_op jit(solution)/shard_map/ppermute | solution.py:47
  198.9 6.8 %copy-start.6 = (bf16[8,128,128]{1,2,0:T(8,128)(2,1)S(1)}, bf16[8,128,128]{1,2,0:T(8,128)(2,1)}, u32[]{:S(2)}) copy-start(bf16[8,128,128]{1,2,0:T(8,128)(2,1)} %copy-done.5) | copy-start | bytes 786436
  198.9 13.8 %collective-permute-start.11 = (bf16[128,1024]{1,0:T(8,128)(2,1)S(1)}, bf16[128,1024]{1,0:T(8,128)(2,1)S(1)}, u32[]{:S(2)}, u32[]{:S(2)}) collective-permute-start(bf16[128,1024]{1,0:T(8,128)(2,1)S(1)} %add_convert_fusion.5), channel_id=1, source_target_pairs={{2,0},{4,2},{6,4},{8,6},{10,8},{12,10},{14,12},{16,14},{18,16},{20... | collective-permute-start | bytes 786440 | tf_op jit(solution)/shard_map/ppermute | solution.py:47
  203.7 2.4 %copy-start.22 = (bf16[8,128,128]{1,2,0:T(8,128)(2,1)S(1)}, bf16[8,128,128]{1,2,0:T(8,128)(2,1)}, u32[]{:S(2)}) copy-start(bf16[8,128,128]{1,2,0:T(8,128)(2,1)} %get-tuple-element.43) | copy-start | bytes 786436
  203.7 13.8 %collective-permute-start.15 = (bf16[128,1024]{1,0:T(8,128)(2,1)S(1)}, bf16[128,1024]{1,0:T(8,128)(2,1)S(1)}, u32[]{:S(2)}, u32[]{:S(2)}) collective-permute-start(bf16[128,1024]{1,0:T(8,128)(2,1)S(1)} %add_convert_fusion.1), channel_id=1, source_target_pairs={{2,0},{4,2},{6,4},{8,6},{10,8},{12,10},{14,12},{16,14},{18,16},{20... | collective-permute-start | bytes 786440 | tf_op jit(solution)/shard_map/ppermute | solution.py:47
  (17 other events, 19.4 us)
